TPU v7x, 32 devices: a whole 2x2x4 slice. The times are simulated.
32 devices in a mesh: gx: 4 (over z), gy: 2 (over y), gz: 4 (over x, core).
Axes of the slice: x: 2, y: 2, z: 4, core: 2. Of those that a mesh axis runs over, the one named last changes fastest.
Arguments:
- positions: float32 [3, 8, 4, 32, 128], P(None, 'gx', 'gy', 'gz'), may hold values from 0 to 1
- shield: float32 [8, 4, 32, 128], P('gx', 'gy', 'gz'), may hold values from 0.3 to 1
- width: float32 [8, 4, 32, 128], P('gx', 'gy', 'gz'), may hold values from 0.5 to 2
- hardness: float32 [8, 4, 32, 128], P('gx', 'gy', 'gz'), may hold values from 0.5 to 2
- softness: float32 [8, 4, 32, 128], P('gx', 'gy', 'gz'), may hold values from 0.5 to 2
- coupling: float32 [8, 4, 32, 128], P('gx', 'gy', 'gz'), may hold values from -0.45 to 0.45
- pair_bits: int32 [8, 4, 32], P('gx', 'gy', 'gz'), may hold values from 8192 to 134217727
- right_side: float32 [4, 8, 4, 32, 128], P(None, 'gx', 'gy', 'gz'), may hold values from -7 to 7
Outputs:
- solution: float32 [4, 8, 4, 32, 128], P(None, 'gx', 'gy', 'gz')
- residual: float32 [4, 8, 4, 32, 128], P(None, 'gx', 'gy', 'gz')
All inputs are finite; a program needn't handle non-finite values.
Results may differ from a plain program's by a relative error of at most 0.0018.
Values sent between devices are 32-bit elements; how exact they have to be, the bound alone decides.
No kernel may reach another device: no remote copies, remote signals or barrier semaphores. Data moves between devices by JAX's collectives and lax.ppermute only.
A program may use at most 128 MiB of HBM per device.

v0:
```python
import jax
import jax.numpy as jnp
from jax import lax
from jax.sharding import PartitionSpec as P

ITERS = 3
coulomb_scale = 0.002
response_scale = 0.003


def extended(block, sides, width):
    for axis, dim in sides:
        count = lax.axis_size(axis)
        forward = [(i, i + 1) for i in range(count - 1)]
        backward = [(target, source) for source, target in forward]
        low = lax.ppermute(
            lax.slice_in_dim(block, block.shape[dim] - width, None, axis=dim), axis, forward
        )
        high = lax.ppermute(lax.slice_in_dim(block, 0, width, axis=dim), axis, backward)
        block = jnp.concatenate([low, block, high], axis=dim)
    return block


def index_tuple(values):
    return tuple((jnp.asarray(value).astype(jnp.int32) for value in values))


def pair_terms(own_params, partner, offset_code, own_bits):
    shift_first = (offset_code // 9 - 1).astype(jnp.float32)
    shift_second = (offset_code // 3 % 3 - 1).astype(jnp.float32)
    shift_third = (offset_code % 3 - 1).astype(jnp.float32)

    def separation(column, shift):
        return shift + (partner[column][:, None, :] - own_params[column][:, :, None])

    first = separation(0, shift_first)
    second = separation(1, shift_second)
    third = separation(2, shift_third)
    distance = first * first + second * second + third * third
    coulomb = coulomb_scale * lax.rsqrt(
        distance + own_params[3][:, :, None] * partner[3][:, None, :]
    )
    response = response_scale * jnp.exp(
        -distance / (own_params[4][:, :, None] + partner[4][:, None, :])
    )
    listed = jnp.right_shift(own_bits, offset_code) & 1 > 0
    tile_size = own_params.shape[2]
    diagonal_mask = lax.broadcasted_iota(
        jnp.int32, (tile_size, tile_size), 0
    ) == lax.broadcasted_iota(jnp.int32, (tile_size, tile_size), 1)
    kept = listed[:, None, None] & jnp.logical_not(diagonal_mask[None] & (offset_code == 13))
    empty_pair = jnp.zeros_like(distance)
    return (
        jnp.where(kept, coulomb, empty_pair).astype(jnp.bfloat16),
        jnp.where(kept, response, empty_pair).astype(jnp.bfloat16),
    )


def tile_block(padded, offset_code, extent):
    fields = padded.shape[0]
    tile_size = padded.shape[4]
    start = index_tuple((0, offset_code // 9, offset_code // 3 % 3, offset_code % 3, 0))
    block = lax.dynamic_slice(padded, start, (fields, extent[0], extent[1], extent[2], tile_size))
    return block.reshape(fields, extent[0] * extent[1] * extent[2], tile_size)


def static_block(padded, offset_code, extent):
    first = offset_code // 9
    second = offset_code // 3 % 3
    third = offset_code % 3
    block = padded[
        :, first : first + extent[0], second : second + extent[1], third : third + extent[2]
    ]
    return block.reshape(padded.shape[0], extent[0] * extent[1] * extent[2], padded.shape[4])


def spread_ghosts(vector, extent):
    shaped = vector.reshape(4, extent[0], extent[1], extent[2], vector.shape[2])
    return extended(shaped, (("gx", 1), ("gy", 2), ("gz", 3)), 1)


def split_parts(padded):
    upper = padded.astype(jnp.bfloat16)
    lower = (padded - upper.astype(jnp.float32)).astype(jnp.bfloat16)
    return jnp.concatenate([upper[:2], lower[:2], upper[2:], lower[2:]], axis=0)


def inner_local(vector, other_vector):
    return jnp.sum((vector * other_vector).reshape(2, 2, -1), axis=(0, 2))


def two_products(vector, applied):
    return lax.psum((inner_local(vector, vector), inner_local(vector, applied)), ("gx", "gy", "gz"))


def widen(scalars):
    return jnp.concatenate([scalars, scalars]).reshape(4, 1, 1)


def on_device(positions, shield, width, hardness, softness, coupling, pair_bits, right_side):
    tiles_x, tiles_y, tiles_z, tile_size = hardness.shape
    extent = (tiles_x, tiles_y, tiles_z)
    tile_count = tiles_x * tiles_y * tiles_z
    params = jnp.concatenate([positions, shield[None], width[None]], axis=0)
    joined = extended(
        jnp.concatenate([params, right_side], axis=0), (("gx", 1), ("gy", 2), ("gz", 3)), 1
    )
    params_pad = joined[:5]
    first_pad = joined[5:]
    own_params = params_pad[:, 1:-1, 1:-1, 1:-1].reshape(5, tile_count, tile_size)
    own_bits = pair_bits.reshape(tile_count)

    def build(offset_code, carry):
        store_coulomb, store_response, row_coulomb, row_response = carry
        offset_code = offset_code.astype(jnp.int32)
        partner = tile_block(params_pad, offset_code, extent)
        coulomb, response = pair_terms(own_params, partner, offset_code, own_bits)
        store_coulomb = lax.dynamic_update_index_in_dim(store_coulomb, coulomb, offset_code, 0)
        store_response = lax.dynamic_update_index_in_dim(store_response, response, offset_code, 0)
        row_coulomb = row_coulomb + jnp.sum(coulomb.astype(jnp.float32), axis=2)
        row_response = row_response + jnp.sum(response.astype(jnp.float32), axis=2)
        return (store_coulomb, store_response, row_coulomb, row_response)

    store_zeros = jnp.zeros((27, tile_count, tile_size, tile_size), jnp.bfloat16)
    flat_zeros = jnp.zeros((tile_count, tile_size), jnp.float32)
    store_coulomb, store_response, row_coulomb, row_response = lax.fori_loop(
        0, 27, build, (store_zeros, store_zeros, flat_zeros, flat_zeros)
    )
    diagonal_charge = hardness.reshape(tile_count, tile_size) + row_coulomb
    diagonal_potential = softness.reshape(tile_count, tile_size) + row_response
    linking = coupling.reshape(tile_count, tile_size)

    def operate(padded, vector):
        parts_pad = split_parts(padded)
        stacked = jnp.stack(
            [static_block(parts_pad, offset_code, extent) for offset_code in range(27)], axis=0
        )
        charge_terms = jnp.einsum(
            "otij,oftj->fti", store_coulomb, stacked[:, :4], preferred_element_type=jnp.float32
        )
        potential_terms = jnp.einsum(
            "otij,oftj->fti", store_response, stacked[:, 4:], preferred_element_type=jnp.float32
        )
        pair_charge = charge_terms[:2] + charge_terms[2:]
        pair_potential = potential_terms[:2] + potential_terms[2:]
        image_charge = diagonal_charge * vector[:2] + pair_charge + linking * vector[2:]
        image_potential = diagonal_potential * vector[2:] - pair_potential + linking * vector[:2]
        return jnp.concatenate([image_charge, image_potential], axis=0)

    rhs_flat = right_side.reshape(4, tile_count, tile_size)
    solution = jnp.zeros_like(rhs_flat)
    applied = operate(first_pad, rhs_flat)
    norm_now, product = two_products(rhs_flat, applied)
    step_size = norm_now / product
    remainder = rhs_flat
    direction = rhs_flat
    along = applied
    for iteration in range(ITERS):
        solution = solution + widen(step_size) * direction
        remainder = remainder - widen(step_size) * along
        if iteration + 1 < ITERS:
            applied = operate(spread_ghosts(remainder, extent), remainder)
            norm_next, product = two_products(remainder, applied)
            beta_ratio = norm_next / norm_now
            step_size = norm_next / (product - beta_ratio * norm_next / step_size)
            direction = remainder + widen(beta_ratio) * direction
            along = applied + widen(beta_ratio) * along
            norm_now = norm_next
    final_image = operate(spread_ghosts(solution, extent), solution)
    residual = rhs_flat - final_image
    shape_out = (4, tiles_x, tiles_y, tiles_z, tile_size)
    return (solution.reshape(shape_out), residual.reshape(shape_out))


def solution(mesh):
    return jax.shard_map(
        on_device,
        mesh=mesh,
        in_specs=(
            P(None, "gx", "gy", "gz", None),
            P("gx", "gy", "gz", None),
            P("gx", "gy", "gz", None),
            P("gx", "gy", "gz", None),
            P("gx", "gy", "gz", None),
            P("gx", "gy", "gz", None),
            P("gx", "gy", "gz"),
            P(None, "gx", "gy", "gz", None),
        ),
        out_specs=(P(None, "gx", "gy", "gz", None), P(None, "gx", "gy", "gz", None)),
        check_vma=False,
    )
```

profile of v0, /device:TPU:14, one launch (start us, length us, event | category | flops | bytes accessed | tf_op | source)
XLA Modules:
  0.0 627.6 jit_solution(3941174055811860574)
XLA Ops:
  30.8 282.4 %while.23 = (s32[]{:T(128)}, bf16[27,32,128,128]{3,2,0,1:T(8,128)(2,1)}, bf16[27,32,128,128]{3,2,0,1:T(8,128)(2,1)}, f32[32,128]{1,0:T(8,128)S(1)}, f32[32,128]{...) while((s32[]{:T(128)}, ...), condition=%wide.region_6.7_spmd.clone, body=%wide.region_3.6_spmd.clone.sunk | while | flops 26271884 | bytes 2933673 | solution.py:126
  31.0 5.2 fusion.83
  36.2 5.0 convert_reduce_fusion.3
  41.5 5.2 fusion.83
  46.7 5.0 convert_reduce_fusion.3
  51.9 5.2 fusion.83
  57.2 5.0 convert_reduce_fusion.3
  62.4 5.2 fusion.83
  67.7 5.0 convert_reduce_fusion.3
  72.9 5.2 fusion.83
  78.1 5.0 convert_reduce_fusion.3
  83.4 5.3 fusion.83
  88.6 5.0 convert_reduce_fusion.3
  93.9 5.2 fusion.83
  99.1 5.0 convert_reduce_fusion.3
  104.3 5.2 fusion.83
  109.6 5.0 convert_reduce_fusion.3
  114.8 5.2 fusion.83
  120.0 5.0 convert_reduce_fusion.3
  125.3 5.2 fusion.83
  130.4 5.0 convert_reduce_fusion.3
  135.7 5.2 fusion.83
  140.9 5.0 convert_reduce_fusion.3
  146.2 5.2 fusion.83
  151.4 5.0 convert_reduce_fusion.3
  156.6 5.2 fusion.83
  161.8 5.0 convert_reduce_fusion.3
  167.0 5.2 fusion.83
  172.2 5.0 convert_reduce_fusion.3
  177.5 5.2 fusion.83
  182.7 5.0 convert_reduce_fusion.3
  187.9 5.2 fusion.83
  193.1 5.0 convert_reduce_fusion.3
  198.4 5.2 fusion.83
  203.6 5.0 convert_reduce_fusion.3
  208.8 5.2 fusion.83
  214.0 5.0 convert_reduce_fusion.3
  219.3 5.2 fusion.83
  224.5 5.0 convert_reduce_fusion.3
  229.8 5.2 fusion.83
  235.0 5.0 convert_reduce_fusion.3
  240.2 5.3 fusion.83
  245.5 5.0 convert_reduce_fusion.3
  250.7 5.3 fusion.83
  256.0 5.0 convert_reduce_fusion.3
  261.2 5.2 fusion.83
  266.4 5.0 convert_reduce_fusion.3
  271.7 5.2 fusion.83
  276.9 5.0 convert_reduce_fusion.3
  282.2 5.2 fusion.83
  287.3 5.0 convert_reduce_fusion.3
  292.6 5.2 fusion.83
  303.0 5.2 fusion.83
  315.7 13.1 %convolution_bitcast_fusion.6 = f32[4,32,128]{2,0,1:T(4,128)S(1)} fusion(bf16[27,32,128,128]{3,2,0,1:T(8,128)(2,1)} %get-tuple-element.243, bf16[27,8,32,128]{3,1,0,2:T(8,128)(2,1)S(1)} %constant_dynamic-update-slice_fusion), kind=kOutput, calls=%fused_computation.39 | convolution fusion | flops 113246208 | bytes 29261824 | tf_op jit(solution)/shard_map/otij,oftj->fti/dot_general | solution.py:141
  328.8 13.4 %convolution_bitcast_fusion.7 = f32[4,32,128]{2,0,1:T(4,128)S(1)} fusion(bf16[27,32,128,128]{3,2,0,1:T(8,128)(2,1)} %get-tuple-element.241, bf16[27,8,32,128]{3,1,0,2:T(8,128)(2,1)S(1)} %constant_dynamic-update-slice_fusion), kind=kOutput, calls=%fused_computation.40 | convolution fusion | flops 113246208 | bytes 29261824 | tf_op jit(solution)/shard_map/otij,oftj->fti/dot_general | solution.py:138
  342.7 39.7 %all-reduce.2 = (f32[2]{0:T(128)S(1)}, f32[2]{0:T(128)S(1)}) all-reduce(f32[2]{0:T(128)S(1)} %reduce_sum.132, f32[2]{0:T(128)S(1)} %reduce_sum.135), channel_id=1, replica_groups=mesh['gx'=4,'gy'=2,'gz'=4] {'gx','gy','gz'}, use_global_device_ids=true, to_apply=%region_2.3 | all-reduce | flops 4 | bytes 32 | tf_op jit(solution)/shard_map/psum | solution.py:93
  410.7 13.1 %convolution_bitcast_fusion.4 = f32[4,32,128]{2,0,1:T(4,128)S(1)} fusion(bf16[27,32,128,128]{3,2,0,1:T(8,128)(2,1)} %get-tuple-element.243, bf16[27,8,32,128]{3,1,0,2:T(8,128)(2,1)S(1)} %constant_dynamic-update-slice_fusion.29), kind=kOutput, calls=%fused_computation.37 | convolution fusion | flops 113246208 | bytes 29261824 | tf_op jit(solution)/shard_map/otij,oftj->fti/dot_general | solution.py:141
  423.8 13.4 %convolution_bitcast_fusion.5 = f32[4,32,128]{2,0,1:T(4,128)S(1)} fusion(bf16[27,32,128,128]{3,2,0,1:T(8,128)(2,1)} %get-tuple-element.241, bf16[27,8,32,128]{3,1,0,2:T(8,128)(2,1)S(1)} %constant_dynamic-update-slice_fusion.29), kind=kOutput, calls=%fused_computation.38 | convolution fusion | flops 113246208 | bytes 29261824 | tf_op jit(solution)/shard_map/otij,oftj->fti/dot_general | solution.py:138
  437.5 39.5 %all-reduce.1 = (f32[2]{0:T(128)S(1)}, f32[2]{0:T(128)S(1)}) all-reduce(f32[2]{0:T(128)S(1)} %reduce_sum.138, f32[2]{0:T(128)S(1)} %reduce_sum.141), channel_id=1, replica_groups=mesh['gx'=4,'gy'=2,'gz'=4] {'gx','gy','gz'}, use_global_device_ids=true, to_apply=%region_12.13 | all-reduce | flops 4 | bytes 32 | tf_op jit(solution)/shard_map/psum | solution.py:93
  505.6 13.4 %convolution_bitcast_fusion.3 = f32[4,32,128]{2,0,1:T(4,128)S(1)} fusion(bf16[27,32,128,128]{3,2,0,1:T(8,128)(2,1)} %get-tuple-element.241, bf16[27,8,32,128]{3,1,0,2:T(8,128)(2,1)S(1)} %constant_dynamic-update-slice_fusion.58), kind=kOutput, calls=%fused_computation.36 | convolution fusion | flops 113246208 | bytes 29261824 | tf_op jit(solution)/shard_map/otij,oftj->fti/dot_general | solution.py:138
  519.0 13.1 %convolution_bitcast_fusion.2 = f32[4,32,128]{2,0,1:T(4,128)S(1)} fusion(bf16[27,32,128,128]{3,2,0,1:T(8,128)(2,1)} %get-tuple-element.243, bf16[27,8,32,128]{3,1,0,2:T(8,128)(2,1)S(1)} %constant_dynamic-update-slice_fusion.58), kind=kOutput, calls=%fused_computation.35 | convolution fusion | flops 113246208 | bytes 29261824 | tf_op jit(solution)/shard_map/otij,oftj->fti/dot_general | solution.py:141
  532.4 39.6 %all-reduce = (f32[2]{0:T(128)S(1)}, f32[2]{0:T(128)S(1)}) all-reduce(f32[2]{0:T(128)S(1)} %reduce_sum.144, f32[2]{0:T(128)S(1)} %reduce_sum.147), channel_id=1, replica_groups=mesh['gx'=4,'gy'=2,'gz'=4] {'gx','gy','gz'}, use_global_device_ids=true, to_apply=%region_18.19 | all-reduce | flops 4 | bytes 32 | tf_op jit(solution)/shard_map/psum | solution.py:93
  600.4 13.4 %convolution_bitcast_fusion.1 = f32[4,32,128]{2,0,1:T(4,128)S(1)} fusion(bf16[27,32,128,128]{3,2,0,1:T(8,128)(2,1)} %get-tuple-element.241, bf16[27,8,32,128]{3,1,0,2:T(8,128)(2,1)S(1)} %constant_dynamic-update-slice_fusion.85), kind=kOutput, calls=%fused_computation.34 | convolution fusion | flops 113246208 | bytes 29261824 | tf_op jit(solution)/shard_map/otij,oftj->fti/dot_general | solution.py:138
  613.8 13.1 %convolution_bitcast_fusion = f32[4,32,128]{2,0,1:T(4,128)S(1)} fusion(bf16[27,32,128,128]{3,2,0,1:T(8,128)(2,1)} %get-tuple-element.243, bf16[27,8,32,128]{3,1,0,2:T(8,128)(2,1)S(1)} %constant_dynamic-update-slice_fusion.85), kind=kOutput, calls=%fused_computation.33 | convolution fusion | flops 113246208 | bytes 29261824 | tf_op jit(solution)/shard_map/otij,oftj->fti/dot_general | solution.py:141
  (522 shorter events, 130.0 us)
Async XLA Ops:
  0.6 14.3 %copy-start = (f32[4,2,2,8,128]{4,3,2,1,0:T(8,128)S(1)}, f32[4,2,2,8,128]{4,3,2,1,0:T(8,128)}, u32[]{:S(2)}) copy-start(f32[4,2,2,8,128]{4,3,2,1,0:T(8,128)} %param.17) | copy-start | bytes 196612
  0.6 20.0 %copy-start.4 = (f32[2,2,8,128]{3,2,1,0:T(8,128)S(1)}, f32[2,2,8,128]{3,2,1,0:T(8,128)}, u32[]{:S(2)}) copy-start(f32[2,2,8,128]{3,2,1,0:T(8,128)} %param.12) | copy-start | bytes 49156
  0.7 20.0 %copy-start.5 = (f32[2,2,8,128]{3,2,1,0:T(8,128)S(1)}, f32[2,2,8,128]{3,2,1,0:T(8,128)}, u32[]{:S(2)}) copy-start(f32[2,2,8,128]{3,2,1,0:T(8,128)} %param.11) | copy-start | bytes 49156
  0.7 20.0 %copy-start.3 = (f32[3,2,2,8,128]{4,3,2,1,0:T(8,128)S(1)}, f32[3,2,2,8,128]{4,3,2,1,0:T(8,128)}, u32[]{:S(2)}) copy-start(f32[3,2,2,8,128]{4,3,2,1,0:T(8,128)} %param.10) | copy-start | bytes 147460
  1.6 6.7 %collective-permute-start.1 = (f32[9,1,2,8,128]{4,3,2,1,0:T(8,128)S(1)}, f32[9,1,2,8,128]{4,3,2,1,0:T(8,128)S(1)}, u32[]{:S(2)}, u32[]{:S(2)}) collective-permute-start(f32[9,1,2,8,128]{4,3,2,1,0:T(8,128)S(1)} %get-tuple-element.453), channel_id=1, source_target_pairs={{8,0},{16,8},{24,16},{9,1},{17,9},{25,17},{10,2},{18,10},{26,18},{... | collective-permute-start | bytes 221192 | tf_op jit(solution)/shard_map/ppermute | solution.py:19
  4.0 6.2 collective-permute-start
  11.2 5.1 collective-permute-start.3
  13.6 7.0 %collective-permute-start.2 = (f32[9,4,1,8,128]{4,3,2,1,0:T(8,128)S(1)}, f32[9,4,1,8,128]{4,3,2,1,0:T(8,128)S(1)}, u32[]{:S(2)}, u32[]{:S(2)}) collective-permute-start(f32[9,4,1,8,128]{4,3,2,1,0:T(8,128)S(1)} %get-tuple-element.428), channel_id=1, source_target_pairs={{0,4},{1,5},{2,6},{3,7},{8,12},{9,13},{10,14},{11,15},{16,20},{17,... | collective-permute-start | bytes 442376 | tf_op jit(solution)/shard_map/ppermute | solution.py:16
  20.8 4.4 collective-permute-start.5
  22.7 5.7 collective-permute-start.4
  28.6 1.0 copy-start.1
  29.7 1.1 slice-start
  328.8 13.4 %copy-start.8 = (f32[2,2,8,128]{3,2,1,0:T(8,128)S(1)}, f32[2,2,8,128]{3,2,1,0:T(8,128)}, u32[]{:S(2)}) copy-start(f32[2,2,8,128]{3,2,1,0:T(8,128)} %param.14) | copy-start | bytes 49156
  328.8 13.4 %copy-start.9 = (f32[2,2,8,128]{3,2,1,0:T(8,128)S(1)}, f32[2,2,8,128]{3,2,1,0:T(8,128)}, u32[]{:S(2)}) copy-start(f32[2,2,8,128]{3,2,1,0:T(8,128)} %param.13) | copy-start | bytes 49156
  328.8 13.4 %copy-start.6 = (f32[2,2,8,128]{3,2,1,0:T(8,128)S(1)}, f32[2,2,8,128]{3,2,1,0:T(8,128)}, u32[]{:S(2)}) copy-start(f32[2,2,8,128]{3,2,1,0:T(8,128)} %param.15) | copy-start | bytes 49156
  328.8 13.4 %copy-start.7 = (f32[2,2,2,8,128]{4,0,3,2,1:T(2,128)S(1)}, f32[2,2,2,8,128]{4,0,3,2,1:T(2,128)}, u32[]{:S(2)}) copy-start(f32[2,2,2,8,128]{4,0,3,2,1:T(2,128)} %copy.141) | copy-start | bytes 98308
  382.7 5.9 collective-permute-start.7
  385.2 5.8 collective-permute-start.6
  391.0 5.7 collective-permute-start.9
  394.9 6.2 collective-permute-start.8
  401.1 4.7 collective-permute-start.11
  403.0 5.2 collective-permute-start.10
  477.5 5.9 collective-permute-start.13
  480.1 5.8 collective-permute-start.12
  486.0 5.7 collective-permute-start.15
  489.8 6.2 collective-permute-start.14
  496.0 4.4 collective-permute-start.17
  497.9 5.2 collective-permute-start.16
  572.3 26.1 %copy-start.2 = (f32[4,2,2,8,128]{4,3,2,1,0:T(8,128)}, f32[4,2,2,8,128]{4,3,2,1,0:T(8,128)S(1)}, u32[]{:S(2)}) copy-start(f32[4,2,2,8,128]{4,3,2,1,0:T(8,128)S(1)} %multiply_add_fusion.2) | copy-start | bytes 196612
  572.3 5.9 collective-permute-start.19
  574.9 5.8 collective-permute-start.18
  580.8 5.7 collective-permute-start.21
  584.6 6.2 collective-permute-start.20
  590.8 4.5 collective-permute-start.23
  592.7 5.2 collective-permute-start.22
where the time goes:
time: 629 us; the launch traced here: 628 us
  other arithmetic  283 us (45%)
  blocking collectives  119 us (19%)
  matrix products  106 us (17%)
  starting transfers between devices  59.9 us (10%)
  waiting for transfers between devices  40.2 us (6%)
  local copies, waits for them, and re-layouts  12.7 us (2%)
    dynamic_update_slice x27, other arithmetic, build(): lax.dynamic_update_index_in_dim(store_response, response, offset_code, 0)  141 us
    reduce_sum x27, other arithmetic, build(): row_response = row_response + jnp.sum(response.astype(jnp.float32), axis=2)  135 us
    psum x3, blocking collectives, two_products(): lax.psum((inner_local(vector, vector), inner_local(vector, applied)), ('g...  119 us
    dot_general x4, matrix products, operate(): jnp.einsum('otij,oftj->fti', store_coulomb, stacked[:, :4], preferred_ele...  53.5 us
    dot_general x4, matrix products, operate(): jnp.einsum('otij,oftj->fti', store_response, stacked[:, 4:], preferred_el...  52.3 us
    ppermute x12, waiting for transfers between devices, extended(): lax.ppermute(lax.slice_in_dim(block, block.shape[dim] - width, None, axis...  37.8 us
    ppermute x12, starting transfers between devices, extended(): lax.ppermute(lax.slice_in_dim(block, 0, width, axis=dim), axis, backward)  31.7 us
    ppermute x12, starting transfers between devices, extended(): lax.ppermute(lax.slice_in_dim(block, block.shape[dim] - width, None, axis...  28.2 us
  transfers between devices with their start and end apart: 24, of which 16 were waited for; matrix products, arithmetic and copies ran while one was open for 0% of the time, Pallas kernels for 0%

commit v1 on v0

--- a/solution.py
+++ b/solution.py
@@ -2,10 +2,12 @@
 import jax.numpy as jnp
 from jax import lax
 from jax.sharding import PartitionSpec as P
+from jax.lax import psum
 
 ITERS = 3
 coulomb_scale = 0.002
 response_scale = 0.003
+assign_thing = lambda block_in: psum(psum(block_in, ("gy", "gz")), "gx")
 
 
 def extended(block, sides, width):
@@ -90,7 +92,7 @@
 
 
 def two_products(vector, applied):
-    return lax.psum((inner_local(vector, vector), inner_local(vector, applied)), ("gx", "gy", "gz"))
+    return assign_thing((inner_local(vector, vector), inner_local(vector, applied)))
 
 
 def widen(scalars):

time: 629 us -> 568 us (0.903)
  blocking collectives: 119 us -> 55.8 us
  waiting for transfers between devices: 40.2 us -> 47.7 us
    psum x3 -> x6, blocking collectives: 119 us -> 55.8 us  [assign_thing = lambda block_in: psum(psum(block_in, ('gy', 'gz')), 'gx')]
    ppermute x12, waiting for transfers between devices: 37.8 us -> 45.3 us  [extended(): lax.ppermute(lax.slice_in_dim(block, block.shape[dim] - width, None, axis...]
where the time goes in v1:
time: 568 us; the launch traced here: 566 us
  other arithmetic  283 us (50%)
  matrix products  105 us (18%)
  blocking collectives  55.8 us (10%)
  starting transfers between devices  54.7 us (10%)
  waiting for transfers between devices  47.7 us (8%)
  local copies, waits for them, and re-layouts  12.7 us (2%)
    dynamic_update_slice x27, other arithmetic, build(): lax.dynamic_update_index_in_dim(store_response, response, offset_code, 0)  141 us
    reduce_sum x27, other arithmetic, build(): row_response = row_response + jnp.sum(response.astype(jnp.float32), axis=2)  135 us
    psum x6, blocking collectives, assign_thing = lambda block_in: psum(psum(block_in, ('gy', 'gz')), 'gx')  55.8 us
    dot_general x4, matrix products, operate(): jnp.einsum('otij,oftj->fti', store_response, stacked[:, 4:], preferred_el...  52.7 us
    dot_general x4, matrix products, operate(): jnp.einsum('otij,oftj->fti', store_coulomb, stacked[:, :4], preferred_ele...  52.4 us
    ppermute x12, waiting for transfers between devices, extended(): lax.ppermute(lax.slice_in_dim(block, block.shape[dim] - width, None, axis...  45.3 us
    ppermute x12, starting transfers between devices, extended(): lax.ppermute(lax.slice_in_dim(block, 0, width, axis=dim), axis, backward)  30.5 us
    ppermute x12, starting transfers between devices, extended(): lax.ppermute(lax.slice_in_dim(block, block.shape[dim] - width, None, axis...  24.2 us
  transfers between devices with their start and end apart: 24, of which 16 were waited for; matrix products, arithmetic and copies ran while one was open for 0% of the time, Pallas kernels for 0%

profile of v1, /device:TPU:14, one launch (start us, length us, event | category | flops | bytes accessed | tf_op | source)
XLA Modules:
  0.0 566.4 jit_solution(12287271475754004539)
XLA Ops:
  30.9 282.5 %while.23 = (s32[]{:T(128)}, bf16[27,32,128,128]{3,2,0,1:T(8,128)(2,1)}, bf16[27,32,128,128]{3,2,0,1:T(8,128)(2,1)}, f32[32,128]{1,0:T(8,128)S(1)}, f32[32,128]{...) while((s32[]{:T(128)}, ...), condition=%wide.region_7.8_spmd.clone, body=%wide.region_4.7_spmd.clone.sunk | while | flops 26271884 | bytes 2933673 | solution.py:128
  31.0 5.2 fusion.83
  36.2 5.0 convert_reduce_fusion.3
  41.4 5.2 fusion.83
  46.7 5.0 convert_reduce_fusion.3
  51.9 5.3 fusion.83
  57.2 5.0 convert_reduce_fusion.3
  62.4 5.2 fusion.83
  67.7 5.0 convert_reduce_fusion.3
  72.9 5.2 fusion.83
  78.1 5.0 convert_reduce_fusion.3
  83.4 5.2 fusion.83
  88.6 5.0 convert_reduce_fusion.3
  93.9 5.2 fusion.83
  99.1 5.0 convert_reduce_fusion.3
  104.4 5.2 fusion.83
  109.6 5.0 convert_reduce_fusion.3
  114.8 5.3 fusion.83
  120.1 5.0 convert_reduce_fusion.3
  125.3 5.2 fusion.83
  130.5 5.0 convert_reduce_fusion.3
  135.8 5.2 fusion.83
  141.0 5.0 convert_reduce_fusion.3
  146.2 5.2 fusion.83
  151.4 5.0 convert_reduce_fusion.3
  156.7 5.2 fusion.83
  161.9 5.0 convert_reduce_fusion.3
  167.1 5.2 fusion.83
  172.3 5.0 convert_reduce_fusion.3
  177.6 5.2 fusion.83
  182.8 5.0 convert_reduce_fusion.3
  188.0 5.2 fusion.83
  193.2 5.0 convert_reduce_fusion.3
  198.5 5.2 fusion.83
  203.7 5.0 convert_reduce_fusion.3
  208.9 5.2 fusion.83
  214.1 5.0 convert_reduce_fusion.3
  219.3 5.2 fusion.83
  229.8 5.2 fusion.83
  240.3 5.2 fusion.83
  245.5 5.0 convert_reduce_fusion.3
  250.7 5.2 fusion.83
  261.2 5.2 fusion.83
  271.6 5.3 fusion.83
  276.9 5.0 convert_reduce_fusion.3
  282.1 5.3 fusion.83
  292.6 5.2 fusion.83
  297.9 5.0 convert_reduce_fusion.3
  303.1 5.2 fusion.83
  315.9 13.2 %convolution_bitcast_fusion.6 = f32[4,32,128]{2,0,1:T(4,128)S(1)} fusion(bf16[27,32,128,128]{3,2,0,1:T(8,128)(2,1)} %get-tuple-element.243, bf16[27,8,32,128]{3,1,0,2:T(8,128)(2,1)S(1)} %constant_dynamic-update-slice_fusion), kind=kOutput, calls=%fused_computation.39 | convolution fusion | flops 113246208 | bytes 29261824 | tf_op jit(solution)/shard_map/otij,oftj->fti/dot_general | solution.py:143
  329.1 13.1 %convolution_bitcast_fusion.7 = f32[4,32,128]{2,0,1:T(4,128)S(1)} fusion(bf16[27,32,128,128]{3,2,0,1:T(8,128)(2,1)} %get-tuple-element.241, bf16[27,8,32,128]{3,1,0,2:T(8,128)(2,1)S(1)} %constant_dynamic-update-slice_fusion), kind=kOutput, calls=%fused_computation.40 | convolution fusion | flops 113246208 | bytes 29261824 | tf_op jit(solution)/shard_map/otij,oftj->fti/dot_general | solution.py:140
  342.7 10.3 %all-reduce.2 = (f32[2]{0:T(128)S(1)}, f32[2]{0:T(128)S(1)}) all-reduce(f32[2]{0:T(128)S(1)} %reduce_sum.132, f32[2]{0:T(128)S(1)} %reduce_sum.135), channel_id=1, replica_groups=mesh['gx'=4,'gy'=2,'gz'=4] {'gy','gz'}, use_global_device_ids=true, to_apply=%region_2.3 | all-reduce | flops 4 | bytes 32 | tf_op jit(solution)/shard_map/psum | solution.py:10
  353.0 9.0 %all-reduce.5 = (f32[2]{0:T(128)S(1)}, f32[2]{0:T(128)S(1)}) all-reduce(f32[2]{0:T(128)S(1)} %get-tuple-element.295, f32[2]{0:T(128)S(1)} %get-tuple-element.296), channel_id=1, replica_groups=mesh['gx'=4,'gy'=2,'gz'=4] {'gx'}, use_global_device_ids=true, to_apply=%region_3.4 | all-reduce | flops 4 | bytes 32 | tf_op jit(solution)/shard_map/psum | solution.py:10
  362.3 5.3 collective-permute-start.7
  392.1 13.2 %convolution_bitcast_fusion.4 = f32[4,32,128]{2,0,1:T(4,128)S(1)} fusion(bf16[27,32,128,128]{3,2,0,1:T(8,128)(2,1)} %get-tuple-element.243, bf16[27,8,32,128]{3,1,0,2:T(8,128)(2,1)S(1)} %constant_dynamic-update-slice_fusion.29), kind=kOutput, calls=%fused_computation.37 | convolution fusion | flops 113246208 | bytes 29261824 | tf_op jit(solution)/shard_map/otij,oftj->fti/dot_general | solution.py:143
  405.3 13.1 %convolution_bitcast_fusion.5 = f32[4,32,128]{2,0,1:T(4,128)S(1)} fusion(bf16[27,32,128,128]{3,2,0,1:T(8,128)(2,1)} %get-tuple-element.241, bf16[27,8,32,128]{3,1,0,2:T(8,128)(2,1)S(1)} %constant_dynamic-update-slice_fusion.29), kind=kOutput, calls=%fused_computation.38 | convolution fusion | flops 113246208 | bytes 29261824 | tf_op jit(solution)/shard_map/otij,oftj->fti/dot_general | solution.py:140
  418.7 10.3 %all-reduce.1 = (f32[2]{0:T(128)S(1)}, f32[2]{0:T(128)S(1)}) all-reduce(f32[2]{0:T(128)S(1)} %reduce_sum.138, f32[2]{0:T(128)S(1)} %reduce_sum.141), channel_id=1, replica_groups=mesh['gx'=4,'gy'=2,'gz'=4] {'gy','gz'}, use_global_device_ids=true, to_apply=%region_14.15 | all-reduce | flops 4 | bytes 32 | tf_op jit(solution)/shard_map/psum | solution.py:10
  429.0 8.0 %all-reduce.4 = (f32[2]{0:T(128)S(1)}, f32[2]{0:T(128)S(1)}) all-reduce(f32[2]{0:T(128)S(1)} %get-tuple-element.293, f32[2]{0:T(128)S(1)} %get-tuple-element.294), channel_id=1, replica_groups=mesh['gx'=4,'gy'=2,'gz'=4] {'gx'}, use_global_device_ids=true, to_apply=%region_15.16 | all-reduce | flops 4 | bytes 32 | tf_op jit(solution)/shard_map/psum | solution.py:10
  465.7 13.1 %convolution_bitcast_fusion.3 = f32[4,32,128]{2,0,1:T(4,128)S(1)} fusion(bf16[27,32,128,128]{3,2,0,1:T(8,128)(2,1)} %get-tuple-element.241, bf16[27,8,32,128]{3,1,0,2:T(8,128)(2,1)S(1)} %constant_dynamic-update-slice_fusion.58), kind=kOutput, calls=%fused_computation.36 | convolution fusion | flops 113246208 | bytes 29261824 | tf_op jit(solution)/shard_map/otij,oftj->fti/dot_general | solution.py:140
  478.8 13.2 %convolution_bitcast_fusion.2 = f32[4,32,128]{2,0,1:T(4,128)S(1)} fusion(bf16[27,32,128,128]{3,2,0,1:T(8,128)(2,1)} %get-tuple-element.243, bf16[27,8,32,128]{3,1,0,2:T(8,128)(2,1)S(1)} %constant_dynamic-update-slice_fusion.58), kind=kOutput, calls=%fused_computation.35 | convolution fusion | flops 113246208 | bytes 29261824 | tf_op jit(solution)/shard_map/otij,oftj->fti/dot_general | solution.py:143
  492.3 10.3 %all-reduce = (f32[2]{0:T(128)S(1)}, f32[2]{0:T(128)S(1)}) all-reduce(f32[2]{0:T(128)S(1)} %reduce_sum.144, f32[2]{0:T(128)S(1)} %reduce_sum.147), channel_id=1, replica_groups=mesh['gx'=4,'gy'=2,'gz'=4] {'gy','gz'}, use_global_device_ids=true, to_apply=%region_22.23 | all-reduce | flops 4 | bytes 32 | tf_op jit(solution)/shard_map/psum | solution.py:10
  502.6 8.0 %all-reduce.3 = (f32[2]{0:T(128)S(1)}, f32[2]{0:T(128)S(1)}) all-reduce(f32[2]{0:T(128)S(1)} %get-tuple-element.291, f32[2]{0:T(128)S(1)} %get-tuple-element.292), channel_id=1, replica_groups=mesh['gx'=4,'gy'=2,'gz'=4] {'gx'}, use_global_device_ids=true, to_apply=%region_23.24 | all-reduce | flops 4 | bytes 32 | tf_op jit(solution)/shard_map/psum | solution.py:10
  539.4 13.1 %convolution_bitcast_fusion.1 = f32[4,32,128]{2,0,1:T(4,128)S(1)} fusion(bf16[27,32,128,128]{3,2,0,1:T(8,128)(2,1)} %get-tuple-element.241, bf16[27,8,32,128]{3,1,0,2:T(8,128)(2,1)S(1)} %constant_dynamic-update-slice_fusion.85), kind=kOutput, calls=%fused_computation.34 | convolution fusion | flops 113246208 | bytes 29261824 | tf_op jit(solution)/shard_map/otij,oftj->fti/dot_general | solution.py:140
  552.5 13.2 %convolution_bitcast_fusion = f32[4,32,128]{2,0,1:T(4,128)S(1)} fusion(bf16[27,32,128,128]{3,2,0,1:T(8,128)(2,1)} %get-tuple-element.243, bf16[27,8,32,128]{3,1,0,2:T(8,128)(2,1)S(1)} %constant_dynamic-update-slice_fusion.85), kind=kOutput, calls=%fused_computation.33 | convolution fusion | flops 113246208 | bytes 29261824 | tf_op jit(solution)/shard_map/otij,oftj->fti/dot_general | solution.py:143
  (525 shorter events, 147.0 us)
Async XLA Ops:
  0.6 14.3 %copy-start = (f32[4,2,2,8,128]{4,3,2,1,0:T(8,128)S(1)}, f32[4,2,2,8,128]{4,3,2,1,0:T(8,128)}, u32[]{:S(2)}) copy-start(f32[4,2,2,8,128]{4,3,2,1,0:T(8,128)} %param.17) | copy-start | bytes 196612
  0.6 20.0 %copy-start.4 = (f32[2,2,8,128]{3,2,1,0:T(8,128)S(1)}, f32[2,2,8,128]{3,2,1,0:T(8,128)}, u32[]{:S(2)}) copy-start(f32[2,2,8,128]{3,2,1,0:T(8,128)} %param.12) | copy-start | bytes 49156
  0.7 20.0 %copy-start.5 = (f32[2,2,8,128]{3,2,1,0:T(8,128)S(1)}, f32[2,2,8,128]{3,2,1,0:T(8,128)}, u32[]{:S(2)}) copy-start(f32[2,2,8,128]{3,2,1,0:T(8,128)} %param.11) | copy-start | bytes 49156
  0.7 20.0 %copy-start.3 = (f32[3,2,2,8,128]{4,3,2,1,0:T(8,128)S(1)}, f32[3,2,2,8,128]{4,3,2,1,0:T(8,128)}, u32[]{:S(2)}) copy-start(f32[3,2,2,8,128]{4,3,2,1,0:T(8,128)} %param.10) | copy-start | bytes 147460
  1.6 6.7 %collective-permute-start.1 = (f32[9,1,2,8,128]{4,3,2,1,0:T(8,128)S(1)}, f32[9,1,2,8,128]{4,3,2,1,0:T(8,128)S(1)}, u32[]{:S(2)}, u32[]{:S(2)}) collective-permute-start(f32[9,1,2,8,128]{4,3,2,1,0:T(8,128)S(1)} %get-tuple-element.459), channel_id=1, source_target_pairs={{8,0},{16,8},{24,16},{9,1},{17,9},{25,17},{10,2},{18,10},{26,18},{... | collective-permute-start | bytes 221192 | tf_op jit(solution)/shard_map/ppermute | solution.py:21
  4.0 6.2 %collective-permute-start = (f32[9,1,2,8,128]{4,3,2,1,0:T(8,128)S(1)}, f32[9,1,2,8,128]{4,3,2,1,0:T(8,128)S(1)}, u32[]{:S(2)}, u32[]{:S(2)}) collective-permute-start(f32[9,1,2,8,128]{4,3,2,1,0:T(8,128)S(1)} %get-tuple-element.458), channel_id=1, source_target_pairs={{0,8},{8,16},{16,24},{1,9},{9,17},{17,25},{2,10},{10,18},{18,26},{... | collective-permute-start | bytes 221192 | tf_op jit(solution)/shard_map/ppermute | solution.py:18
  11.2 5.1 collective-permute-start.3
  13.6 7.0 %collective-permute-start.2 = (f32[9,4,1,8,128]{4,3,2,1,0:T(8,128)S(1)}, f32[9,4,1,8,128]{4,3,2,1,0:T(8,128)S(1)}, u32[]{:S(2)}, u32[]{:S(2)}) collective-permute-start(f32[9,4,1,8,128]{4,3,2,1,0:T(8,128)S(1)} %get-tuple-element.434), channel_id=1, source_target_pairs={{0,4},{1,5},{2,6},{3,7},{8,12},{9,13},{10,14},{11,15},{16,20},{17,... | collective-permute-start | bytes 442376 | tf_op jit(solution)/shard_map/ppermute | solution.py:18
  20.8 4.4 collective-permute-start.5
  22.7 5.7 %collective-permute-start.4 = (f32[9,4,4,1,128]{4,3,2,1,0:T(1,128)S(1)}, f32[9,4,4,1,128]{4,3,2,1,0:T(1,128)S(1)}, u32[]{:S(2)}, u32[]{:S(2)}) collective-permute-start(f32[9,4,4,1,128]{4,3,2,1,0:T(1,128)S(1)} %get-tuple-element.324), channel_id=1, source_target_pairs={{0,1},{1,2},{2,3},{4,5},{5,6},{6,7},{8,9},{9,10},{10,11},{12,13},{... | collective-permute-start | bytes 221192 | tf_op jit(solution)/shard_map/ppermute | solution.py:18
  28.6 1.0 copy-start.1
  29.7 1.1 slice-start
  329.0 13.2 %copy-start.8 = (f32[2,2,8,128]{3,2,1,0:T(8,128)S(1)}, f32[2,2,8,128]{3,2,1,0:T(8,128)}, u32[]{:S(2)}) copy-start(f32[2,2,8,128]{3,2,1,0:T(8,128)} %param.14) | copy-start | bytes 49156
  329.0 13.2 %copy-start.9 = (f32[2,2,8,128]{3,2,1,0:T(8,128)S(1)}, f32[2,2,8,128]{3,2,1,0:T(8,128)}, u32[]{:S(2)}) copy-start(f32[2,2,8,128]{3,2,1,0:T(8,128)} %param.13) | copy-start | bytes 49156
  329.0 13.2 %copy-start.6 = (f32[2,2,8,128]{3,2,1,0:T(8,128)S(1)}, f32[2,2,8,128]{3,2,1,0:T(8,128)}, u32[]{:S(2)}) copy-start(f32[2,2,8,128]{3,2,1,0:T(8,128)} %param.15) | copy-start | bytes 49156
  329.1 13.2 %copy-start.7 = (f32[2,2,2,8,128]{4,0,3,2,1:T(2,128)S(1)}, f32[2,2,2,8,128]{4,0,3,2,1:T(2,128)}, u32[]{:S(2)}) copy-start(f32[2,2,2,8,128]{4,0,3,2,1:T(2,128)} %copy.141) | copy-start | bytes 98308
  362.3 7.3 %collective-permute-start.7 = (f32[4,1,2,8,128]{4,3,2,1,0:T(8,128)S(1)}, f32[4,1,2,8,128]{4,3,2,1,0:T(8,128)S(1)}, u32[]{:S(2)}, u32[]{:S(2)}) collective-permute-start(f32[4,1,2,8,128]{4,3,2,1,0:T(8,128)S(1)} %get-tuple-element.483), channel_id=1, source_target_pairs={{8,0},{16,8},{24,16},{9,1},{17,9},{25,17},{10,2},{18,10},{26,18},{... | collective-permute-start | bytes 98312 | tf_op jit(solution)/shard_map/ppermute | solution.py:21
  367.6 5.8 %collective-permute-start.6 = (f32[4,1,2,8,128]{4,3,2,1,0:T(8,128)S(1)}, f32[4,1,2,8,128]{4,3,2,1,0:T(8,128)S(1)}, u32[]{:S(2)}, u32[]{:S(2)}) collective-permute-start(f32[4,1,2,8,128]{4,3,2,1,0:T(8,128)S(1)} %get-tuple-element.482), channel_id=1, source_target_pairs={{0,8},{8,16},{16,24},{1,9},{9,17},{17,25},{2,10},{10,18},{18,26},{... | collective-permute-start | bytes 98312 | tf_op jit(solution)/shard_map/ppermute | solution.py:18
  373.4 3.2 collective-permute-start.9
  374.8 6.2 %collective-permute-start.8 = (f32[4,4,1,8,128]{4,3,2,1,0:T(8,128)S(1)}, f32[4,4,1,8,128]{4,3,2,1,0:T(8,128)S(1)}, u32[]{:S(2)}, u32[]{:S(2)}) collective-permute-start(f32[4,4,1,8,128]{4,3,2,1,0:T(8,128)S(1)} %get-tuple-element.464), channel_id=1, source_target_pairs={{0,4},{1,5},{2,6},{3,7},{8,12},{9,13},{10,14},{11,15},{16,20},{17,... | collective-permute-start | bytes 196616 | tf_op jit(solution)/shard_map/ppermute | solution.py:18
  381.0 4.7 collective-permute-start.11
  382.9 6.8 %collective-permute-start.10 = (f32[4,4,4,1,128]{4,3,2,1,0:T(1,128)S(1)}, f32[4,4,4,1,128]{4,3,2,1,0:T(1,128)S(1)}, u32[]{:S(2)}, u32[]{:S(2)}) collective-permute-start(f32[4,4,4,1,128]{4,3,2,1,0:T(1,128)S(1)} %get-tuple-element.452), channel_id=1, source_target_pairs={{0,1},{1,2},{2,3},{4,5},{5,6},{6,7},{8,9},{9,10},{10,11},{12,13},{... | collective-permute-start | bytes 98312 | tf_op jit(solution)/shard_map/ppermute | solution.py:18
  437.5 6.2 %collective-permute-start.13 = (f32[4,1,2,8,128]{4,3,2,1,0:T(8,128)S(1)}, f32[4,1,2,8,128]{4,3,2,1,0:T(8,128)S(1)}, u32[]{:S(2)}, u32[]{:S(2)}) collective-permute-start(f32[4,1,2,8,128]{4,3,2,1,0:T(8,128)S(1)} %get-tuple-element.481), channel_id=1, source_target_pairs={{8,0},{16,8},{24,16},{9,1},{17,9},{25,17},{10,2},{18,10},{26,18},{... | collective-permute-start | bytes 98312 | tf_op jit(solution)/shard_map/ppermute | solution.py:21
  441.8 5.8 %collective-permute-start.12 = (f32[4,1,2,8,128]{4,3,2,1,0:T(8,128)S(1)}, f32[4,1,2,8,128]{4,3,2,1,0:T(8,128)S(1)}, u32[]{:S(2)}, u32[]{:S(2)}) collective-permute-start(f32[4,1,2,8,128]{4,3,2,1,0:T(8,128)S(1)} %get-tuple-element.480), channel_id=1, source_target_pairs={{0,8},{8,16},{16,24},{1,9},{9,17},{17,25},{2,10},{10,18},{18,26},{... | collective-permute-start | bytes 98312 | tf_op jit(solution)/shard_map/ppermute | solution.py:18
  447.6 3.2 collective-permute-start.15
  448.9 6.2 %collective-permute-start.14 = (f32[4,4,1,8,128]{4,3,2,1,0:T(8,128)S(1)}, f32[4,4,1,8,128]{4,3,2,1,0:T(8,128)S(1)}, u32[]{:S(2)}, u32[]{:S(2)}) collective-permute-start(f32[4,4,1,8,128]{4,3,2,1,0:T(8,128)S(1)} %get-tuple-element.462), channel_id=1, source_target_pairs={{0,4},{1,5},{2,6},{3,7},{8,12},{9,13},{10,14},{11,15},{16,20},{17,... | collective-permute-start | bytes 196616 | tf_op jit(solution)/shard_map/ppermute | solution.py:18
  455.1 4.4 collective-permute-start.17
  457.1 6.2 %collective-permute-start.16 = (f32[4,4,4,1,128]{4,3,2,1,0:T(1,128)S(1)}, f32[4,4,4,1,128]{4,3,2,1,0:T(1,128)S(1)}, u32[]{:S(2)}, u32[]{:S(2)}) collective-permute-start(f32[4,4,4,1,128]{4,3,2,1,0:T(1,128)S(1)} %get-tuple-element.446), channel_id=1, source_target_pairs={{0,1},{1,2},{2,3},{4,5},{5,6},{6,7},{8,9},{9,10},{10,11},{12,13},{... | collective-permute-start | bytes 98312 | tf_op jit(solution)/shard_map/ppermute | solution.py:18
  510.9 26.5 %copy-start.2 = (f32[4,2,2,8,128]{4,3,2,1,0:T(8,128)}, f32[4,2,2,8,128]{4,3,2,1,0:T(8,128)S(1)}, u32[]{:S(2)}) copy-start(f32[4,2,2,8,128]{4,3,2,1,0:T(8,128)S(1)} %multiply_add_fusion.2) | copy-start | bytes 196612
  510.9 6.2 %collective-permute-start.19 = (f32[4,1,2,8,128]{4,3,2,1,0:T(8,128)S(1)}, f32[4,1,2,8,128]{4,3,2,1,0:T(8,128)S(1)}, u32[]{:S(2)}, u32[]{:S(2)}) collective-permute-start(f32[4,1,2,8,128]{4,3,2,1,0:T(8,128)S(1)} %get-tuple-element.477), channel_id=1, source_target_pairs={{8,0},{16,8},{24,16},{9,1},{17,9},{25,17},{10,2},{18,10},{26,18},{... | collective-permute-start | bytes 98312 | tf_op jit(solution)/shard_map/ppermute | solution.py:21
  515.2 5.8 %collective-permute-start.18 = (f32[4,1,2,8,128]{4,3,2,1,0:T(8,128)S(1)}, f32[4,1,2,8,128]{4,3,2,1,0:T(8,128)S(1)}, u32[]{:S(2)}, u32[]{:S(2)}) collective-permute-start(f32[4,1,2,8,128]{4,3,2,1,0:T(8,128)S(1)} %get-tuple-element.476), channel_id=1, source_target_pairs={{0,8},{8,16},{16,24},{1,9},{9,17},{17,25},{2,10},{10,18},{18,26},{... | collective-permute-start | bytes 98312 | tf_op jit(solution)/shard_map/ppermute | solution.py:18
  521.0 3.2 collective-permute-start.21
  522.4 6.2 %collective-permute-start.20 = (f32[4,4,1,8,128]{4,3,2,1,0:T(8,128)S(1)}, f32[4,4,1,8,128]{4,3,2,1,0:T(8,128)S(1)}, u32[]{:S(2)}, u32[]{:S(2)}) collective-permute-start(f32[4,4,1,8,128]{4,3,2,1,0:T(8,128)S(1)} %get-tuple-element.460), channel_id=1, source_target_pairs={{0,4},{1,5},{2,6},{3,7},{8,12},{9,13},{10,14},{11,15},{16,20},{17,... | collective-permute-start | bytes 196616 | tf_op jit(solution)/shard_map/ppermute | solution.py:18
  528.6 4.7 collective-permute-start.23
  530.7 6.2 %collective-permute-start.22 = (f32[4,4,4,1,128]{4,3,2,1,0:T(1,128)S(1)}, f32[4,4,4,1,128]{4,3,2,1,0:T(1,128)S(1)}, u32[]{:S(2)}, u32[]{:S(2)}) collective-permute-start(f32[4,4,4,1,128]{4,3,2,1,0:T(1,128)S(1)} %get-tuple-element.440), channel_id=1, source_target_pairs={{0,1},{1,2},{2,3},{4,5},{5,6},{6,7},{8,9},{9,10},{10,11},{12,13},{... | collective-permute-start | bytes 98312 | tf_op jit(solution)/shard_map/ppermute | solution.py:18
